TPU v7x, 256 devices: a whole 4x4x8 slice. The times are simulated.
256 devices in a mesh: dp: 64 (over z, x, core), tensor: 4 (over y).
Axes of the slice: x: 4, y: 4, z: 8, core: 2. Of those that a mesh axis runs over, the one named last changes fastest.
Arguments:
- prefix: bfloat16 [64, 128, 8192], P('dp'), may hold values from -6 to 6
- kv_weight: bfloat16 [8192, 2, 512], P(None, None, 'tensor'), may hold values from -0.044194174 to 0.044194174
- ans_query: bfloat16 [65536, 4096], P('dp', 'tensor'), may hold values from -60 to 60
- ans_kv: bfloat16 [65536, 2, 512], P('dp', None, 'tensor'), may hold values from -8 to 8
- d_out: bfloat16 [65536, 4096], P('dp', 'tensor'), may hold values from -192 to 192
- branch_prompt: int32 [128], P('dp'), may hold values from 0 to 63, as said below
Outputs:
- attn_out: bfloat16 [65536, 4096], P('dp', 'tensor')
- prefix_grad: bfloat16 [64, 128, 8192], P('dp', 'tensor')
Inputs may be any that keep to these rules, and one draw needn't show every extreme that they name: `branch_prompt`: prompt p is owned by dp index p. The dp index that holds a branch and the owner of its prompt are at most 3 steps apart, counting around the axis. Every dp index holds at least one answer to its own prompt.
All inputs are finite; a program needn't handle non-finite values.
Results may differ from a plain program's by a relative error of at most 0.014.
The roundings to bfloat16 on the way count: a program that leaves them out, or rounds other values in their place, can miss the bound.
Values may be sent and summed in bfloat16 or wider, within the bound.
A program may use at most 128 MiB of HBM per device.

v0:
```python
import jax
import jax.numpy as jnp
from jax import lax
from jax.sharding import PartitionSpec as P

HD = 128
REACH = 3


def shifted(x, axis, by):
    devices = lax.axis_size(axis)
    return lax.ppermute(x, axis, [(i, (i + by) % devices) for i in range(devices)])


def in_blocks(x, dim, devices):
    shape = x.shape
    parts = x.reshape(*shape[:dim], devices, shape[dim] // devices, *shape[dim + 1 :])
    return jnp.moveaxis(parts, dim, 0)


def sent_and_summed(x, axis, dim):
    parts = in_blocks(x, dim, lax.axis_size(axis))
    arrived = lax.all_to_all(parts, axis, split_axis=0, concat_axis=0, tiled=True)
    return arrived.astype(jnp.float32).sum(axis=0)


def branch_pass(queries, key_rows, value_rows, upstream):
    answers = queries.shape[0]
    prefix_len = key_rows.shape[0] - answers
    scaling = queries.shape[-1] ** (-0.5)
    scores = (
        jnp.einsum("ahgd,khd->hgak", queries, key_rows, preferred_element_type=jnp.float32)
        * scaling
    )
    key_pos = jnp.arange(key_rows.shape[0])
    row_pos = jnp.arange(answers)
    allowed = (key_pos[None, :] < prefix_len) | (key_pos[None, :] - prefix_len <= row_pos[:, None])
    scores = jnp.where(allowed, scores, -jnp.inf)
    row_max = jnp.max(scores, axis=-1, keepdims=True)
    exps = jnp.exp(scores - row_max)
    prob_full = exps / jnp.sum(exps, axis=-1, keepdims=True)
    prob_half = prob_full.astype(jnp.bfloat16)
    context = jnp.einsum(
        "hgak,khd->ahgd", prob_half, value_rows, preferred_element_type=jnp.float32
    )
    prob_grad = jnp.einsum(
        "ahgd,khd->hgak", upstream, value_rows, preferred_element_type=jnp.float32
    )
    delta_row = jnp.einsum("ahgd,ahgd->hga", upstream, context, preferred_element_type=jnp.float32)
    score_half = (prob_full * (prob_grad - delta_row[..., None])).astype(jnp.bfloat16)
    key_grad = (
        jnp.einsum(
            "hgak,ahgd->khd",
            score_half[..., :prefix_len],
            queries,
            preferred_element_type=jnp.float32,
        )
        * scaling
    )
    value_grad = jnp.einsum(
        "hgak,ahgd->khd", prob_half[..., :prefix_len], upstream, preferred_element_type=jnp.float32
    )
    return (context.astype(jnp.bfloat16), key_grad, value_grad)


def shards(prefix, kv_weight, ans_query, ans_kv, d_out, branch_prompt):
    prefix_len = prefix.shape[1]
    model_width = prefix.shape[2]
    columns = kv_weight.shape[2]
    heads_here = columns // HD
    groups = ans_query.shape[1] // columns
    branches = branch_prompt.shape[0]
    answers = ans_query.shape[0] // branches
    flat_weight = kv_weight.reshape(kv_weight.shape[0], 2 * columns)
    own_kv = jnp.dot(prefix[0], flat_weight, preferred_element_type=jnp.float32).astype(
        jnp.bfloat16
    )
    my_index = lax.axis_index("dp")
    dp_count = lax.axis_size("dp")
    window = 2 * REACH + 1
    slot_index = (branch_prompt - my_index + REACH) % dp_count
    pieces = [own_kv] * window
    for offset in range(window):
        if offset != REACH:
            pieces[offset] = shifted(own_kv, "dp", REACH - offset)
    nearby = jnp.stack(pieces, axis=0)
    chosen = jnp.take(nearby, slot_index, axis=0).reshape(branches, prefix_len, 2, heads_here, HD)
    queries = ans_query.reshape(branches, answers, heads_here, groups, HD)
    answer_kv = ans_kv.reshape(branches, answers, 2, heads_here, HD)
    upstream = d_out.reshape(branches, answers, heads_here, groups, HD)

    def one_branch(packed):
        branch_q, branch_kv, branch_up, prompt_kv = packed
        key_rows = jnp.concatenate([prompt_kv[:, 0], branch_kv[:, 0]], axis=0)
        value_rows = jnp.concatenate([prompt_kv[:, 1], branch_kv[:, 1]], axis=0)
        return branch_pass(branch_q, key_rows, value_rows, branch_up)

    context, key_grad, value_grad = lax.map(one_branch, (queries, answer_kv, upstream, chosen))
    attn_out = context.reshape(branches * answers, groups * columns)
    both_grads = jnp.stack([key_grad, value_grad], axis=2).reshape(
        branches, prefix_len * 2 * columns
    )
    selector = (slot_index[:, None] == jnp.arange(window)[None, :]).astype(jnp.float32)
    placed = jnp.dot(selector.T, both_grads).reshape(window, prefix_len, 2 * columns)
    kv_sum = placed[REACH]
    for offset in range(window):
        if offset != REACH:
            kv_sum = kv_sum + shifted(
                placed[offset].astype(jnp.bfloat16), "dp", offset - REACH
            ).astype(jnp.float32)
    kv_grad = kv_sum.astype(jnp.bfloat16)
    tensor_count = lax.axis_size("tensor")
    prefix_rows = sent_and_summed(
        lax.dot_general(
            kv_grad, flat_weight, (((1,), (1,)), ((), ())), preferred_element_type=jnp.float32
        ).astype(jnp.bfloat16),
        "tensor",
        0,
    )
    prefix_grad = prefix_rows.astype(jnp.bfloat16).reshape(
        1, prefix_len // tensor_count, model_width
    )
    return (attn_out, prefix_grad)


def solution(mesh):
    return jax.shard_map(
        shards,
        mesh=mesh,
        in_specs=(
            P("dp", None, None),
            P(None, None, "tensor"),
            P("dp", "tensor"),
            P("dp", None, "tensor"),
            P("dp", "tensor"),
            P("dp"),
        ),
        out_specs=(P("dp", "tensor"), P("dp", "tensor", None)),
        check_vma=False,
    )
```

profile of v0, /device:TPU:102, one launch (start us, length us, event | category | flops | bytes accessed | tf_op | source)
XLA Modules:
  0.0 140.7 jit_solution(13949068702194905192)
XLA Ops:
  0.6 0.0 copy-start
  0.7 1.6 %copy-done = bf16[1,128,8192]{2,1,0:T(8,128)(2,1)S(1)} copy-done((bf16[1,128,8192]{2,1,0:T(8,128)(2,1)S(1)}, bf16[1,128,8192]{2,1,0:T(8,128)(2,1)}, u32[]{:S(2)}) %copy-start) | copy-done | bytes 2097176
  2.2 2.9 %fusion.32 = bf16[128,256]{1,0:T(8,128)(2,1)S(1)} fusion(bf16[1024,8,2,128]{3,2,1,0:T(2,128)(2,1)} %bitcast.209, bf16[1,128,8192]{2,1,0:T(8,128)(2,1)S(1)} %copy-done), kind=kOutput, calls=%fused_computation.61 | convolution fusion | flops 536903680 | bytes 6356992 | tf_op jit(solution)/shard_map/dot_general | solution.py:75
  5.1 0.0 copy-start.2
  5.1 2.6 %collective-permute-start = (bf16[128,256]{1,0:T(8,128)(2,1)S(1)}, bf16[128,256]{1,0:T(8,128)(2,1)S(1)}, u32[]{:S(2)}, u32[]{:S(2)}) collective-permute-start(bf16[128,256]{1,0:T(8,128)(2,1)S(1)} %fusion.32), channel_id=1, source_target_pairs={{0,12},{4,16},{8,20},{12,24},{16,28},{20,32},{24,36},{28,40},{32,4... | collective-permute-start | bytes 196616 | tf_op jit(solution)/shard_map/ppermute | solution.py:12
  7.7 1.5 %collective-permute-start.1 = (bf16[128,256]{1,0:T(8,128)(2,1)S(1)}, bf16[128,256]{1,0:T(8,128)(2,1)S(1)}, u32[]{:S(2)}, u32[]{:S(2)}) collective-permute-start(bf16[128,256]{1,0:T(8,128)(2,1)S(1)} %fusion.32), channel_id=1, source_target_pairs={{0,8},{4,12},{8,16},{12,20},{16,24},{20,28},{24,32},{28,36},{32,40... | collective-permute-start | bytes 196616 | tf_op jit(solution)/shard_map/ppermute | solution.py:12
  9.2 1.9 %collective-permute-start.2 = (bf16[128,256]{1,0:T(8,128)(2,1)S(1)}, bf16[128,256]{1,0:T(8,128)(2,1)S(1)}, u32[]{:S(2)}, u32[]{:S(2)}) collective-permute-start(bf16[128,256]{1,0:T(8,128)(2,1)S(1)} %fusion.32), channel_id=1, source_target_pairs={{0,4},{4,8},{8,12},{12,16},{16,20},{20,24},{24,28},{28,32},{32,36}... | collective-permute-start | bytes 196616 | tf_op jit(solution)/shard_map/ppermute | solution.py:12
  11.1 0.0 collective-permute-start.3
  11.1 0.3 collective-permute-start.4
  11.5 3.5 %copy.51 = bf16[128,8,8,128]{3,2,1,0:T(8,128)(2,1)} copy(bf16[128,8,8,128]{3,1,2,0:T(8,128)(2,1)} %bitcast.212) | data formatting | bytes 4194304
  15.1 1.9 %copy.52 = bf16[128,8,8,128]{3,2,1,0:T(8,128)(2,1)} copy(bf16[128,8,8,128]{3,1,2,0:T(8,128)(2,1)S(1)} %bitcast.213) | data formatting | bytes 4194304
  17.0 0.3 collective-permute-start.5
  17.4 2.2 %collective-permute-done.4 = bf16[128,256]{1,0:T(8,128)(2,1)S(1)} collective-permute-done((bf16[128,256]{1,0:T(8,128)(2,1)S(1)}, bf16[128,256]{1,0:T(8,128)(2,1)S(1)}, u32[]{:S(2)}, u32[]{:S(2)}) %collective-permute-start.4) | collective-permute-done | bytes 65568 | tf_op jit(solution)/shard_map/ppermute | solution.py:12
  19.7 5.1 %collective-permute-done.5 = bf16[128,256]{1,0:T(8,128)(2,1)S(1)} collective-permute-done((bf16[128,256]{1,0:T(8,128)(2,1)S(1)}, bf16[128,256]{1,0:T(8,128)(2,1)S(1)}, u32[]{:S(2)}, u32[]{:S(2)}) %collective-permute-start.5) | collective-permute-done | bytes 65568 | tf_op jit(solution)/shard_map/ppermute | solution.py:12
  24.8 0.6 gather_fusion
  25.4 0.1 copy_select_fusion
  25.4 60.2 %while.16 = (s32[]{:T(128)}, bf16[2,512,1,8,128]{4,3,1,0,2:T(8,128)(2,1)}, bf16[2,128,1,128]{1,3,2,0:T(8,128)(2,1)S(1)}, bf16[2,128,1,128]{1,3,2,0:T(8,128)(2,1)...) while((s32[]{:T(128)}, ...), condition=%wide.region_3.4_spmd, body=%wide.region_0.3_spmd.sunk | while | flops 2318472448 | bytes 97214312 | solution.py:98
  25.5 1.7 %constant_dynamic-slice_fusion.5 = (bf16[1,512,1,8,128]{4,3,1,0,2:T(8,128)(2,1)S(1)}, bf16[1,512,1,8,128]{4,3,1,0,2:T(8,128)(2,1)S(1)}) fusion(bf16[2,512,1,8,128]{4,3,1,0,2:T(8,128)(2,1)} %get-tuple-element.254, s32[]{:T(128)} %get-tuple-element.238, bf16[2,512,1,8,128]{4,3,1,0,2:T(8,128)(2,1)} %get-tuple-element.253), kind=kLoop, calls=%fused_computation.46.clone.1 | loop fusion | bytes 4194308 | tf_op jit(solution)/shard_map/while/body/jit(dynamic_index_in_dim)/dynamic_slice | solution.py:98
  27.1 1.1 constant_dynamic-slice_fusion.6
  28.4 0.3 fusion.60
  28.7 1.9 %fusion.61 = (f32[8,512]{1,0:T(8,128)S(1)}, f32[640,512,8]{1,0,2:T(8,128)S(1)}) fusion(pred[512,640]{0,1:T(8,128)(4,1)S(1)} %fusion.60, bf16[1,512,1,8,128]{4,3,1,0,2:T(8,128)(2,1)S(1)} %get-tuple-element.218, bf16[512,1,128]{2,0,1:T(8,128)(2,1)S(1)} %get-tuple-element.219, bf16[128,1,128]{2,0,1:T(8,128)(2,1)S(1)} %get-tuple-element.220), kind=kOutput, calls=%fused_computation.5.clone.1 | convolution fusion | flops 679276544 | bytes 12042240 | tf_op jit(solution)/shard_map/while/body/eval_jaxpr/ahgd,khd->hgak/dot_general | solution.py:32
  30.6 2.1 %fusion.62 = f32[8,512]{1,0:T(8,128)S(1)} fusion(f32[640,512,8]{1,0,2:T(8,128)S(1)} %get-tuple-element.221, f32[8,512]{1,0:T(8,128)S(1)} %get-tuple-element.222, pred[512,640]{0,1:T(8,128)(4,1)S(1)} %fusion.60), kind=kLoop, calls=%fused_computation.4.clone.1 | loop fusion | flops 10481664 | bytes 10846208 | tf_op jit(solution)/shard_map/while/body/eval_jaxpr/reduce_sum | solution.py:41
  32.8 6.6 %fusion.63 = (bf16[1,8,512,640]{2,3,1,0:T(8,128)(2,1)}, f32[1,8,512,640]{2,3,1,0:T(8,128)}) fusion(f32[8,512]{1,0:T(8,128)S(1)} %fusion.62, f32[8,512]{1,0:T(8,128)S(1)} %get-tuple-element.222, f32[640,512,8]{1,0,2:T(8,128)S(1)} %get-tuple-element.221, pred[512,640]{0,1:T(8,128)(4,1)S(1)} %fusion.60), kind=kLoop, calls=%fused_computation.90.clone.1 | loop fusion | flops 13107200 | bytes 26574848 | tf_op jit(solution)/shard_map/while/body/eval_jaxpr/convert_element_type | solution.py:42
  39.3 1.5 %bitcast_convert_fusion.3 = f32[8,512,128]{2,1,0:T(8,128)} fusion(bf16[1,512,1,8,128]{4,3,1,0,2:T(8,128)(2,1)S(1)} %get-tuple-element.217), kind=kLoop, calls=%fused_computation.28.clone.1 | loop fusion | flops 524288 | bytes 3145728 | tf_op jit(solution)/shard_map/while
  40.8 2.9 %copy.96 = f32[8,512,128]{1,2,0:T(8,128)} copy(f32[8,512,128]{2,1,0:T(8,128)} %bitcast_convert_fusion.3) | data formatting | bytes 4194304 | tf_op jit(solution)/shard_map/while
  43.8 4.2 %fusion.64 = (f32[8,512]{1,0:T(8,128)S(1)}, bf16[128,8,512]{2,0,1:T(8,128)(2,1)S(1)}) fusion(f32[8,512,128]{1,2,0:T(8,128)} %copy.96, bf16[1,8,512,640]{2,3,1,0:T(8,128)(2,1)} %get-tuple-element.223, bf16[512,1,128]{2,0,1:T(8,128)(2,1)S(1)} %get-tuple-element.224, bf16[128,1,128]{2,0,1:T(8,128)(2,1)S(1)} %get-tuple-element.225), kind=kOutput, calls=%fused_computation.13.clone.1 | convolution fusion | flops 672985088 | bytes 8568832 | tf_op jit(solution)/shard_map/while/body/eval_jaxpr/hgak,khd->ahgd/dot_general | solution.py:43
  48.0 1.5 %convolution_bitcast_fusion.4 = f32[1,8,512,640]{2,3,1,0:T(8,128)S(1)} fusion(bf16[1,512,1,8,128]{4,3,1,0,2:T(8,128)(2,1)S(1)} %get-tuple-element.217, bf16[512,1,128]{2,0,1:T(8,128)(2,1)S(1)} %get-tuple-element.224, bf16[128,1,128]{2,0,1:T(8,128)(2,1)S(1)} %get-tuple-element.225), kind=kOutput, calls=%fused_computation.8.clone.1 | convolution fusion | flops 671416320 | bytes 11698176 | tf_op jit(solution)/shard_map/while/body/eval_jaxpr/ahgd,khd->hgak/dot_general | solution.py:46
  49.5 2.3 %fusion.66 = bf16[2,128,1,128]{1,3,2,0:T(8,128)(2,1)S(1)} fusion(bf16[2,128,1,128]{1,3,2,0:T(8,128)(2,1)S(1)} %get-tuple-element.240, s32[]{:T(128)} %get-tuple-element.238, f32[1,8,512,640]{2,3,1,0:T(8,128)S(1)} %convolution_bitcast_fusion.4, f32[1,8,512,640]{2,3,1,0:T(8,128)} %get-tuple-element.227, f32[8,512]{1,0:T(8,128)S(1)} %get-tuple-element.228, ...), kind=kOutput, calls=%fused_computation.22.clone.1 | convolution fusion | flops 135806976 | bytes 5325312 | tf_op jit(solution)/shard_map/while/body/eval_jaxpr/hgak,ahgd->khd/dot_general | solution.py:52
  51.8 0.1 fusion.65
  51.8 0.8 copy.98
  52.6 1.1 constant_dynamic-update-slice_fusion.2
  53.7 1.7 %fusion.67 = bf16[2,128,1,128]{1,3,2,0:T(8,128)(2,1)S(1)} fusion(bf16[2,128,1,128]{1,3,2,0:T(8,128)(2,1)S(1)} %get-tuple-element.241, s32[]{:T(128)} %get-tuple-element.238, bf16[1,8,512,640]{2,3,1,0:T(8,128)(2,1)} %get-tuple-element.223, bf16[1,512,1,8,128]{4,3,1,0,2:T(8,128)(2,1)S(1)} %get-tuple-element.217), kind=kOutput, calls=%fused_computation.18.clone.1 | convolution fusion | flops 134217728 | bytes 2163200 | tf_op jit(solution)/shard_map/while/body/eval_jaxpr/hgak,ahgd->khd/dot_general | solution.py:60
  55.5 1.7 %constant_dynamic-slice_fusion.5 = (bf16[1,512,1,8,128]{4,3,1,0,2:T(8,128)(2,1)S(1)}, bf16[1,512,1,8,128]{4,3,1,0,2:T(8,128)(2,1)S(1)}) fusion(bf16[2,512,1,8,128]{4,3,1,0,2:T(8,128)(2,1)} %get-tuple-element.254, s32[]{:T(128)} %get-tuple-element.238, bf16[2,512,1,8,128]{4,3,1,0,2:T(8,128)(2,1)} %get-tuple-element.253), kind=kLoop, calls=%fused_computation.46.clone.1 | loop fusion | bytes 4194308 | tf_op jit(solution)/shard_map/while/body/jit(dynamic_index_in_dim)/dynamic_slice | solution.py:98
  57.1 1.1 constant_dynamic-slice_fusion.6
  58.4 0.3 fusion.60
  58.7 1.9 %fusion.61 = (f32[8,512]{1,0:T(8,128)S(1)}, f32[640,512,8]{1,0,2:T(8,128)S(1)}) fusion(pred[512,640]{0,1:T(8,128)(4,1)S(1)} %fusion.60, bf16[1,512,1,8,128]{4,3,1,0,2:T(8,128)(2,1)S(1)} %get-tuple-element.218, bf16[512,1,128]{2,0,1:T(8,128)(2,1)S(1)} %get-tuple-element.219, bf16[128,1,128]{2,0,1:T(8,128)(2,1)S(1)} %get-tuple-element.220), kind=kOutput, calls=%fused_computation.5.clone.1 | convolution fusion | flops 679276544 | bytes 12042240 | tf_op jit(solution)/shard_map/while/body/eval_jaxpr/ahgd,khd->hgak/dot_general | solution.py:32
  60.6 2.1 %fusion.62 = f32[8,512]{1,0:T(8,128)S(1)} fusion(f32[640,512,8]{1,0,2:T(8,128)S(1)} %get-tuple-element.221, f32[8,512]{1,0:T(8,128)S(1)} %get-tuple-element.222, pred[512,640]{0,1:T(8,128)(4,1)S(1)} %fusion.60), kind=kLoop, calls=%fused_computation.4.clone.1 | loop fusion | flops 10481664 | bytes 10846208 | tf_op jit(solution)/shard_map/while/body/eval_jaxpr/reduce_sum | solution.py:41
  62.7 6.6 %fusion.63 = (bf16[1,8,512,640]{2,3,1,0:T(8,128)(2,1)}, f32[1,8,512,640]{2,3,1,0:T(8,128)}) fusion(f32[8,512]{1,0:T(8,128)S(1)} %fusion.62, f32[8,512]{1,0:T(8,128)S(1)} %get-tuple-element.222, f32[640,512,8]{1,0,2:T(8,128)S(1)} %get-tuple-element.221, pred[512,640]{0,1:T(8,128)(4,1)S(1)} %fusion.60), kind=kLoop, calls=%fused_computation.90.clone.1 | loop fusion | flops 13107200 | bytes 26574848 | tf_op jit(solution)/shard_map/while/body/eval_jaxpr/convert_element_type | solution.py:42
  69.3 1.5 %bitcast_convert_fusion.3 = f32[8,512,128]{2,1,0:T(8,128)} fusion(bf16[1,512,1,8,128]{4,3,1,0,2:T(8,128)(2,1)S(1)} %get-tuple-element.217), kind=kLoop, calls=%fused_computation.28.clone.1 | loop fusion | flops 524288 | bytes 3145728 | tf_op jit(solution)/shard_map/while
  70.8 2.9 %copy.96 = f32[8,512,128]{1,2,0:T(8,128)} copy(f32[8,512,128]{2,1,0:T(8,128)} %bitcast_convert_fusion.3) | data formatting | bytes 4194304 | tf_op jit(solution)/shard_map/while
  73.8 4.2 %fusion.64 = (f32[8,512]{1,0:T(8,128)S(1)}, bf16[128,8,512]{2,0,1:T(8,128)(2,1)S(1)}) fusion(f32[8,512,128]{1,2,0:T(8,128)} %copy.96, bf16[1,8,512,640]{2,3,1,0:T(8,128)(2,1)} %get-tuple-element.223, bf16[512,1,128]{2,0,1:T(8,128)(2,1)S(1)} %get-tuple-element.224, bf16[128,1,128]{2,0,1:T(8,128)(2,1)S(1)} %get-tuple-element.225), kind=kOutput, calls=%fused_computation.13.clone.1 | convolution fusion | flops 672985088 | bytes 8568832 | tf_op jit(solution)/shard_map/while/body/eval_jaxpr/hgak,khd->ahgd/dot_general | solution.py:43
  77.9 1.5 %convolution_bitcast_fusion.4 = f32[1,8,512,640]{2,3,1,0:T(8,128)S(1)} fusion(bf16[1,512,1,8,128]{4,3,1,0,2:T(8,128)(2,1)S(1)} %get-tuple-element.217, bf16[512,1,128]{2,0,1:T(8,128)(2,1)S(1)} %get-tuple-element.224, bf16[128,1,128]{2,0,1:T(8,128)(2,1)S(1)} %get-tuple-element.225), kind=kOutput, calls=%fused_computation.8.clone.1 | convolution fusion | flops 671416320 | bytes 11698176 | tf_op jit(solution)/shard_map/while/body/eval_jaxpr/ahgd,khd->hgak/dot_general | solution.py:46
  79.5 2.3 %fusion.66 = bf16[2,128,1,128]{1,3,2,0:T(8,128)(2,1)S(1)} fusion(bf16[2,128,1,128]{1,3,2,0:T(8,128)(2,1)S(1)} %get-tuple-element.240, s32[]{:T(128)} %get-tuple-element.238, f32[1,8,512,640]{2,3,1,0:T(8,128)S(1)} %convolution_bitcast_fusion.4, f32[1,8,512,640]{2,3,1,0:T(8,128)} %get-tuple-element.227, f32[8,512]{1,0:T(8,128)S(1)} %get-tuple-element.228, ...), kind=kOutput, calls=%fused_computation.22.clone.1 | convolution fusion | flops 135806976 | bytes 5325312 | tf_op jit(solution)/shard_map/while/body/eval_jaxpr/hgak,ahgd->khd/dot_general | solution.py:52
  81.8 0.1 fusion.65
  81.8 0.8 copy.98
  82.6 1.1 constant_dynamic-update-slice_fusion.2
  83.7 1.7 %fusion.67 = bf16[2,128,1,128]{1,3,2,0:T(8,128)(2,1)S(1)} fusion(bf16[2,128,1,128]{1,3,2,0:T(8,128)(2,1)S(1)} %get-tuple-element.241, s32[]{:T(128)} %get-tuple-element.238, bf16[1,8,512,640]{2,3,1,0:T(8,128)(2,1)} %get-tuple-element.223, bf16[1,512,1,8,128]{4,3,1,0,2:T(8,128)(2,1)S(1)} %get-tuple-element.217), kind=kOutput, calls=%fused_computation.18.clone.1 | convolution fusion | flops 134217728 | bytes 2163200 | tf_op jit(solution)/shard_map/while/body/eval_jaxpr/hgak,ahgd->khd/dot_general | solution.py:60
  85.6 0.1 copy.28
  85.8 0.4 fusion.44
  86.2 2.2 %slice_reduce_fusion.5 = (bf16[32768]{0:T(1024)(128)(2,1)S(1)}, bf16[32768]{0:T(1024)(128)(2,1)S(1)}, bf16[32768]{0:T(1024)(128)(2,1)S(1)}, bf16[32768]{0:T(1024...) fusion(bf16[7,32768]{1,0:T(8,128)(2,1)S(1)} %get-tuple-element.152), kind=kLoop, calls=%fused_computation.68 | loop fusion | bytes 786432 | tf_op jit(solution)/shard_map/slice | solution.py:109
  88.5 1.4 %collective-permute-start.10 = (bf16[128,256]{1,0:T(8,128)(2,1)S(1)}, bf16[128,256]{1,0:T(8,128)(2,1)S(1)}, u32[]{:S(2)}, u32[]{:S(2)}) collective-permute-start(bf16[128,256]{1,0:T(8,128)(2,1)S(1)} %convert_element_type.81), channel_id=1, source_target_pairs={{0,8},{4,12},{8,16},{12,20},{16,24},{20,28},{24,32},{28,36},{32,40... | collective-permute-start | bytes 196616 | tf_op jit(solution)/shard_map/ppermute | solution.py:12
  89.9 1.3 collective-permute-start.11
  91.3 2.1 %collective-permute-start.6 = (bf16[128,256]{1,0:T(8,128)(2,1)S(1)}, bf16[128,256]{1,0:T(8,128)(2,1)S(1)}, u32[]{:S(2)}, u32[]{:S(2)}) collective-permute-start(bf16[128,256]{1,0:T(8,128)(2,1)S(1)} %convert_element_type.73), channel_id=1, source_target_pairs={{0,244},{4,248},{8,252},{12,0},{16,4},{20,8},{24,12},{28,16},{32,2... | collective-permute-start | bytes 196616 | tf_op jit(solution)/shard_map/ppermute | solution.py:12
  93.4 0.8 collective-permute-start.7
  94.2 0.1 collective-permute-start.8
  94.3 0.6 collective-permute-start.9
  94.9 0.4 slice_reduce_fusion.6
  95.3 3.1 %collective-permute-done.6 = bf16[128,256]{1,0:T(8,128)(2,1)S(1)} collective-permute-done((bf16[128,256]{1,0:T(8,128)(2,1)S(1)}, bf16[128,256]{1,0:T(8,128)(2,1)S(1)}, u32[]{:S(2)}, u32[]{:S(2)}) %collective-permute-start.6) | collective-permute-done | bytes 65568 | tf_op jit(solution)/shard_map/ppermute | solution.py:12
  98.4 2.6 %collective-permute-done.7 = bf16[128,256]{1,0:T(8,128)(2,1)S(1)} collective-permute-done((bf16[128,256]{1,0:T(8,128)(2,1)S(1)}, bf16[128,256]{1,0:T(8,128)(2,1)S(1)}, u32[]{:S(2)}, u32[]{:S(2)}) %collective-permute-start.7) | collective-permute-done | bytes 65568 | tf_op jit(solution)/shard_map/ppermute | solution.py:12
  101.1 5.0 %convolution_convert_fusion = bf16[128,8192]{1,0:T(8,128)(2,1)} fusion(bf16[1024,8,2,128]{3,2,1,0:T(2,128)(2,1)} %bitcast.210, bf16[128,256]{1,0:T(8,128)(2,1)S(1)} %collective-permute-done.11, bf16[128,256]{1,0:T(8,128)(2,1)S(1)} %collective-permute-done.10, bf16[128,256]{1,0:T(8,128)(2,1)S(1)} %collective-permute-done.9, ...), kind=kOutput, calls=%fused_computation.53 | convolution fusion | flops 538345472 | bytes 6815744 | tf_op jit(solution)/shard_map/dot_general | solution.py:114
  106.0 4.4 %all-to-all-start = ((bf16[4,32,8192]{2,1,0:T(8,128)(2,1)}), bf16[4,32,8192]{2,1,0:T(8,128)(2,1)}, u32[]{:S(2)}, u32[]{:S(2)}) async-start(bf16[4,32,8192]{2,1,0:T(8,128)(2,1)} %bitcast.208), calls=%async_computation | async-start | bytes 4194304 | tf_op jit(solution)/shard_map/all_to_all | solution.py:23
  110.5 3.7 %copy.82 = bf16[128,8,8,128]{3,1,2,0:T(8,128)(2,1)} copy(bf16[128,8,8,128]{3,2,1,0:T(8,128)(2,1)} %bitcast.214) | data formatting | bytes 4194304
  114.2 23.6 %all-to-all-done = bf16[4,32,8192]{2,1,0:T(8,128)(2,1)} async-done(((bf16[4,32,8192]{2,1,0:T(8,128)(2,1)}), bf16[4,32,8192]{2,1,0:T(8,128)(2,1)}, u32[]{:S(2)}, u32[]{:S(2)}) %all-to-all-start) | async-done | bytes 2097184 | tf_op jit(solution)/shard_map/all_to_all | solution.py:23
  137.8 2.8 %reduce_sum.21 = bf16[32,8192]{1,0:T(8,128)(2,1)} reduce(bf16[4,32,8192]{2,1,0:T(8,128)(2,1)} %all-to-all-done, bf16[]{:T(256)} %constant.85.clone.1), dimensions={0}, to_apply=%region_4.5 | reduce | flops 786432 | bytes 2621442 | tf_op jit(solution)/shard_map/reduce_sum | solution.py:24
  (48 shorter events, 0.6 us)
Async XLA Ops:
  0.6 1.6 %copy-start = (bf16[1,128,8192]{2,1,0:T(8,128)(2,1)S(1)}, bf16[1,128,8192]{2,1,0:T(8,128)(2,1)}, u32[]{:S(2)}) copy-start(bf16[1,128,8192]{2,1,0:T(8,128)(2,1)} %param.8) | copy-start | bytes 6291460
  0.6 10.8 %copy-start.3 = (s32[2]{0:T(128)S(1)}, s32[2]{0:T(128)}, u32[]{:S(2)}) copy-start(s32[2]{0:T(128)} %param.13) | copy-start | bytes 28
  5.1 9.9 %copy-start.2 = (bf16[1024,1024]{1,0:T(8,128)(2,1)S(1)}, bf16[1024,1024]{1,0:T(8,128)(2,1)}, u32[]{:S(2)}) copy-start(bf16[1024,1024]{1,0:T(8,128)(2,1)} %param.12) | copy-start | bytes 6291460
  5.1 11.9 %collective-permute-start = (bf16[128,256]{1,0:T(8,128)(2,1)S(1)}, bf16[128,256]{1,0:T(8,128)(2,1)S(1)}, u32[]{:S(2)}, u32[]{:S(2)}) collective-permute-start(bf16[128,256]{1,0:T(8,128)(2,1)S(1)} %fusion.32), channel_id=1, source_target_pairs={{0,12},{4,16},{8,20},{12,24},{16,28},{20,32},{24,36},{28,40},{32,4... | collective-permute-start | bytes 196616 | tf_op jit(solution)/shard_map/ppermute | solution.py:12
  7.7 9.7 %collective-permute-start.1 = (bf16[128,256]{1,0:T(8,128)(2,1)S(1)}, bf16[128,256]{1,0:T(8,128)(2,1)S(1)}, u32[]{:S(2)}, u32[]{:S(2)}) collective-permute-start(bf16[128,256]{1,0:T(8,128)(2,1)S(1)} %fusion.32), channel_id=1, source_target_pairs={{0,8},{4,12},{8,16},{12,20},{16,24},{20,28},{24,32},{28,36},{32,40... | collective-permute-start | bytes 196616 | tf_op jit(solution)/shard_map/ppermute | solution.py:12
  9.2 8.2 %collective-permute-start.2 = (bf16[128,256]{1,0:T(8,128)(2,1)S(1)}, bf16[128,256]{1,0:T(8,128)(2,1)S(1)}, u32[]{:S(2)}, u32[]{:S(2)}) collective-permute-start(bf16[128,256]{1,0:T(8,128)(2,1)S(1)} %fusion.32), channel_id=1, source_target_pairs={{0,4},{4,8},{8,12},{12,16},{16,20},{20,24},{24,28},{28,32},{32,36}... | collective-permute-start | bytes 196616 | tf_op jit(solution)/shard_map/ppermute | solution.py:12
  11.1 6.3 %collective-permute-start.3 = (bf16[128,256]{1,0:T(8,128)(2,1)S(1)}, bf16[128,256]{1,0:T(8,128)(2,1)S(1)}, u32[]{:S(2)}, u32[]{:S(2)}) collective-permute-start(bf16[128,256]{1,0:T(8,128)(2,1)S(1)} %fusion.32), channel_id=1, source_target_pairs={{0,252},{4,0},{8,4},{12,8},{16,12},{20,16},{24,20},{28,24},{32,28}... | collective-permute-start | bytes 196616 | tf_op jit(solution)/shard_map/ppermute | solution.py:12
  11.1 8.5 %collective-permute-start.4 = (bf16[128,256]{1,0:T(8,128)(2,1)S(1)}, bf16[128,256]{1,0:T(8,128)(2,1)S(1)}, u32[]{:S(2)}, u32[]{:S(2)}) collective-permute-start(bf16[128,256]{1,0:T(8,128)(2,1)S(1)} %fusion.32), channel_id=1, source_target_pairs={{0,248},{4,252},{8,0},{12,4},{16,8},{20,12},{24,16},{28,20},{32,24... | collective-permute-start | bytes 196616 | tf_op jit(solution)/shard_map/ppermute | solution.py:12
  17.0 7.7 %collective-permute-start.5 = (bf16[128,256]{1,0:T(8,128)(2,1)S(1)}, bf16[128,256]{1,0:T(8,128)(2,1)S(1)}, u32[]{:S(2)}, u32[]{:S(2)}) collective-permute-start(bf16[128,256]{1,0:T(8,128)(2,1)S(1)} %fusion.32), channel_id=1, source_target_pairs={{0,244},{4,248},{8,252},{12,0},{16,4},{20,8},{24,12},{28,16},{32,2... | collective-permute-start | bytes 196616 | tf_op jit(solution)/shard_map/ppermute | solution.py:12
  88.5 5.8 %collective-permute-start.10 = (bf16[128,256]{1,0:T(8,128)(2,1)S(1)}, bf16[128,256]{1,0:T(8,128)(2,1)S(1)}, u32[]{:S(2)}, u32[]{:S(2)}) collective-permute-start(bf16[128,256]{1,0:T(8,128)(2,1)S(1)} %convert_element_type.81), channel_id=1, source_target_pairs={{0,8},{4,12},{8,16},{12,20},{16,24},{20,28},{24,32},{28,36},{32,40... | collective-permute-start | bytes 196616 | tf_op jit(solution)/shard_map/ppermute | solution.py:12
  89.9 5.4 %collective-permute-start.11 = (bf16[128,256]{1,0:T(8,128)(2,1)S(1)}, bf16[128,256]{1,0:T(8,128)(2,1)S(1)}, u32[]{:S(2)}, u32[]{:S(2)}) collective-permute-start(bf16[128,256]{1,0:T(8,128)(2,1)S(1)} %convert_element_type.83), channel_id=1, source_target_pairs={{0,12},{4,16},{8,20},{12,24},{16,28},{20,32},{24,36},{28,40},{32,4... | collective-permute-start | bytes 196616 | tf_op jit(solution)/shard_map/ppermute | solution.py:12
  91.3 7.2 %collective-permute-start.6 = (bf16[128,256]{1,0:T(8,128)(2,1)S(1)}, bf16[128,256]{1,0:T(8,128)(2,1)S(1)}, u32[]{:S(2)}, u32[]{:S(2)}) collective-permute-start(bf16[128,256]{1,0:T(8,128)(2,1)S(1)} %convert_element_type.73), channel_id=1, source_target_pairs={{0,244},{4,248},{8,252},{12,0},{16,4},{20,8},{24,12},{28,16},{32,2... | collective-permute-start | bytes 196616 | tf_op jit(solution)/shard_map/ppermute | solution.py:12
  93.4 7.7 %collective-permute-start.7 = (bf16[128,256]{1,0:T(8,128)(2,1)S(1)}, bf16[128,256]{1,0:T(8,128)(2,1)S(1)}, u32[]{:S(2)}, u32[]{:S(2)}) collective-permute-start(bf16[128,256]{1,0:T(8,128)(2,1)S(1)} %convert_element_type.75), channel_id=1, source_target_pairs={{0,248},{4,252},{8,0},{12,4},{16,8},{20,12},{24,16},{28,20},{32,24... | collective-permute-start | bytes 196616 | tf_op jit(solution)/shard_map/ppermute | solution.py:12
  94.2 6.9 %collective-permute-start.8 = (bf16[128,256]{1,0:T(8,128)(2,1)S(1)}, bf16[128,256]{1,0:T(8,128)(2,1)S(1)}, u32[]{:S(2)}, u32[]{:S(2)}) collective-permute-start(bf16[128,256]{1,0:T(8,128)(2,1)S(1)} %convert_element_type.77), channel_id=1, source_target_pairs={{0,252},{4,0},{8,4},{12,8},{16,12},{20,16},{24,20},{28,24},{32,28}... | collective-permute-start | bytes 196616 | tf_op jit(solution)/shard_map/ppermute | solution.py:12
  94.3 6.7 %collective-permute-start.9 = (bf16[128,256]{1,0:T(8,128)(2,1)S(1)}, bf16[128,256]{1,0:T(8,128)(2,1)S(1)}, u32[]{:S(2)}, u32[]{:S(2)}) collective-permute-start(bf16[128,256]{1,0:T(8,128)(2,1)S(1)} %convert_element_type.79), channel_id=1, source_target_pairs={{0,4},{4,8},{8,12},{12,16},{16,20},{20,24},{24,28},{28,32},{32,36}... | collective-permute-start | bytes 196616 | tf_op jit(solution)/shard_map/ppermute | solution.py:12
  106.0 31.8 %all-to-all-start = ((bf16[4,32,8192]{2,1,0:T(8,128)(2,1)}), bf16[4,32,8192]{2,1,0:T(8,128)(2,1)}, u32[]{:S(2)}, u32[]{:S(2)}) async-start(bf16[4,32,8192]{2,1,0:T(8,128)(2,1)} %bitcast.208), calls=%async_computation | async-start | bytes 4194304 | tf_op jit(solution)/shard_map/all_to_all | solution.py:23
  110.5 30.2 %copy-start.1 = (bf16[1,128,8192]{2,1,0:T(8,128)(2,1)S(1)}, bf16[1,128,8192]{2,1,0:T(8,128)(2,1)}, u32[]{:S(2)}) copy-start(bf16[1,128,8192]{2,1,0:T(8,128)(2,1)} %param.8) | copy-start | bytes 6291460
where the time goes:
time: 141 us
  waiting for transfers between devices  36.7 us (26%)
  matrix products  31.5 us (22%)
  local copies, waits for them, and re-layouts  29.8 us (21%)
  other arithmetic  24 us (17%)
  starting transfers between devices  17.3 us (12%)
    all_to_all x1, waiting for transfers between devices, sent_and_summed(): lax.all_to_all(parts, axis, split_axis=0, concat_axis=0, tiled=True)  23.6 us
    convert_element_type x2, other arithmetic, branch_pass(): prob_half = prob_full.astype(jnp.bfloat16)  13.2 us
    ppermute x12, waiting for transfers between devices, shifted(): lax.ppermute(x, axis, [(i, (i + by) % devices) for i in range(devices)])  13.1 us
    ppermute x12, starting transfers between devices, shifted(): lax.ppermute(x, axis, [(i, (i + by) % devices) for i in range(devices)])  12.9 us
    unnamed x17, local copies, waits for them, and re-layouts  10.8 us
    dot_general x2, matrix products, branch_pass(): jnp.einsum('hgak,khd->ahgd', prob_half, value_rows, preferred_element_typ...  8.35 us
    while x2, local copies, waits for them, and re-layouts  5.85 us
    dynamic_slice x6, local copies, waits for them, and re-layouts, shards(): lax.map(one_branch, (queries, answer_kv, upstream, chosen))  5.71 us
  transfers between devices with their start and end apart: 13, of which 5 were waited for; matrix products, arithmetic and copies ran while one was open for 7% of the time, Pallas kernels for 0%

commit v1 on v0

v1 whole, which is shorter than its diff:
```python
import functools
import math

import jax
import jax.numpy as jnp
from jax import lax
from jax.experimental import pallas as pl
from jax.experimental.pallas import tpu as pltpu
from jax.sharding import PartitionSpec as P

MESH = pl.DeviceIdType.MESH
HD = 128
PFX = 128
ANS = 512
HEADS = 8
D = 8192
REACH = 3
WINDOW = 2 * REACH + 1
CHUNK = 512
CHUNKS = D // CHUNK
COLS = 1024
ROWS = 256
FIRST = 4
SCALING = HD ** (-0.5)
LOG2E = math.log2(math.e)
OFFSETS = [o for o in (3, -3, 2, -2, 1, -1)]
f32, bf16 = jnp.float32, jnp.bfloat16


def dot(a, b, dims):
    return lax.dot_general(a, b, (dims, ((), ())), preferred_element_type=f32)


def kernel(
    dp_count,
    t_count,
    bp_ref,
    prefix_hbm,
    w_hbm,
    q_hbm,
    kv_hbm,
    do_hbm,
    attn_hbm,
    pg_hbm,
    prefix_v,
    w_v,
    q_v,
    do_v,
    kv_v,
    wide,
    acc,
    near,
    kfull,
    vfull,
    res,
    kg,
    gsend,
    grecv,
    gbuf,
    wbuf,
    wfull,
    otile,
    load_sem,
    in_sem,
    out_sem,
    kv_send,
    kv_recv,
    w_send,
    w_recv,
    gr_send,
    gr_recv,
    gt_send,
    gt_recv,
    pg_send,
    pg_recv,
):
    d = lax.axis_index("dp")
    t = lax.axis_index("tensor")
    core = lax.rem(d, 2)
    sib = d + 1 - 2 * core
    unit = t * 2 + core

    def dp_at(by):
        return lax.rem(d + by + dp_count, dp_count)

    def t_at(by):
        return lax.rem(t + by, t_count)

    loads = []
    for c in range(CHUNKS):
        cols = pl.ds(c * CHUNK, CHUNK)
        rows = pl.ds(c * 2 * CHUNK, 2 * CHUNK)
        pltpu.make_async_copy(prefix_hbm.at[:, cols], prefix_v.at[:, cols], load_sem.at[0, c]).start()
        pltpu.make_async_copy(w_hbm.at[rows], w_v.at[rows], load_sem.at[1, c]).start()
    for n, (src, dst) in enumerate(((kv_hbm, kv_v), (q_hbm, q_v), (do_hbm, do_v))):
        cp = pltpu.make_async_copy(src, dst, in_sem.at[n])
        cp.start()
        loads.append(cp)

    barrier = pltpu.get_barrier_semaphore()
    for o in OFFSETS:
        pl.semaphore_signal(barrier, inc=1, device_id={"dp": dp_at(o), "tensor": t}, device_id_type=MESH)
    for by in range(1, 4):
        pl.semaphore_signal(barrier, inc=1, device_id={"dp": d, "tensor": t_at(by)}, device_id_type=MESH)
        pl.semaphore_signal(barrier, inc=1, device_id={"dp": sib, "tensor": t_at(by)}, device_id_type=MESH)
    pl.semaphore_wait(barrier, 12)

    w_copies = []
    for by in (2, 1, 3):
        to = t_at(by)
        rows = pl.ds(pl.multiple_of((to * 2 + core) * 2 * COLS, 2 * COLS), 2 * COLS)
        cp = pltpu.make_async_remote_copy(
            src_ref=w_hbm.at[rows],
            dst_ref=wbuf.at[by - 1],
            send_sem=w_send.at[by - 1],
            recv_sem=w_recv.at[by - 1],
            device_id={"dp": d, "tensor": to},
            device_id_type=MESH,
        )
        cp.start()
        w_copies.append(cp)

    def halves(block, n):
        wide[pl.ds(0, 2 * n), :] = block.astype(f32)
        even = wide[pl.ds(0, n, stride=2), :].astype(bf16)
        odd = wide[pl.ds(1, n, stride=2), :].astype(bf16)
        return even, odd

    acc[...] = jnp.zeros_like(acc)

    def project(c, carry):
        cols = pl.ds(pl.multiple_of(c * CHUNK, CHUNK), CHUNK)
        rows = pl.ds(pl.multiple_of(c * 2 * CHUNK, 2 * CHUNK), 2 * CHUNK)
        pltpu.make_async_copy(prefix_hbm.at[:, cols], prefix_v.at[:, cols], load_sem.at[0, c]).wait()
        pltpu.make_async_copy(w_hbm.at[rows], w_v.at[rows], load_sem.at[1, c]).wait()
        wk, wv = halves(w_v[rows, :], CHUNK)
        acc[...] += dot(prefix_v[:, cols], jnp.concatenate([wk, wv], axis=1), ((1,), (0,)))
        return carry

    lax.fori_loop(0, CHUNKS, project, 0)
    near[REACH] = acc[...].astype(bf16)

    kv_copies = []
    for n, o in enumerate(OFFSETS):
        cp = pltpu.make_async_remote_copy(
            src_ref=near.at[REACH],
            dst_ref=near.at[REACH - o],
            send_sem=kv_send.at[n],
            recv_sem=kv_recv.at[n],
            device_id={"dp": dp_at(o), "tensor": t},
            device_id_type=MESH,
        )
        cp.start()
        kv_copies.append(cp)

    first_own = bp_ref[0] == d
    own_slot = jnp.where(first_own, 0, 1)
    other_slot = 1 - own_slot
    other_index = lax.rem(jnp.where(first_own, bp_ref[1], bp_ref[0]) - d + REACH + dp_count, dp_count)

    for cp in loads:
        cp.wait()

    def take_answers(role, slot):
        keys, values = halves(kv_v[slot], ANS)
        kfull[role, pl.ds(PFX, ANS), :] = keys
        vfull[role, pl.ds(PFX, ANS), :] = values

    def take_prefix(role, block):
        kfull[role, pl.ds(0, PFX), :] = block[:, :HD]
        vfull[role, pl.ds(0, PFX), :] = block[:, HD:]

    take_answers(0, own_slot)
    take_answers(1, other_slot)
    take_prefix(0, near[REACH])
    kg[...] = jnp.zeros_like(kg)

    def attend(n, carry):
        @pl.when(n == FIRST)
        def _():
            for cp in kv_copies:
                cp.wait()
            take_prefix(1, near[jnp.minimum(other_index, WINDOW - 1)])

        is_other = (n >= FIRST) & (n < FIRST + HEADS)
        role = jnp.where(is_other, 1, 0)
        head = jnp.where(n < FIRST, n, jnp.where(is_other, n - FIRST, n - HEADS))
        slot = jnp.where(is_other, other_slot, own_slot)
        lanes = pl.ds(pl.multiple_of(head * HD, HD), HD)
        for i in range(ANS // ROWS):
            rows = pl.ds(i * ROWS, ROWS)
            keys = PFX + (i + 1) * ROWS
            q = q_v[slot, rows, lanes]
            do = do_v[slot, rows, lanes]
            s = dot(q, kfull[role, pl.ds(0, keys), :], ((1,), (1,)))
            row_at = lax.broadcasted_iota(jnp.int32, (ROWS, ROWS), 0)
            key_at = lax.broadcasted_iota(jnp.int32, (ROWS, ROWS), 1)
            tail = jnp.where(key_at <= row_at, s[:, keys - ROWS :], -jnp.inf)
            s = jnp.concatenate([s[:, : keys - ROWS], tail], axis=1)
            top = jnp.max(s, axis=1, keepdims=True)
            e = jnp.exp2((s - top) * (SCALING * LOG2E))
            full = e * (1.0 / jnp.sum(e, axis=1, keepdims=True))
            half = full.astype(bf16)
            ctx = dot(half, vfull[role, pl.ds(0, keys), :], ((1,), (0,)))
            res[role, rows, lanes] = ctx.astype(bf16)
            grad = dot(do, vfull[role, pl.ds(0, PFX), :], ((1,), (1,)))
            delta = jnp.sum(do.astype(f32) * ctx, axis=1, keepdims=True)
            sg = (full[:, :PFX] * (grad - delta)).astype(bf16)
            kg[role, 0] += dot(sg, q, ((0,), (0,)))
            kg[role, 1] += dot(half[:, :PFX], do, ((0,), (0,)))

        @pl.when(n == FIRST + HEADS - 1)
        def _():
            key_grad = (kg[1, 0] * SCALING).astype(bf16)
            value_grad = kg[1, 1].astype(bf16)
            zero = jnp.zeros((PFX, HD), bf16)
            for m, o in enumerate(OFFSETS):
                keep = other_index == o + REACH
                gsend[m, :, pl.ds(0, HD)] = lax.select(keep, key_grad, zero)
                gsend[m, :, pl.ds(HD, HD)] = lax.select(keep, value_grad, zero)
                grad_copy(m, o).start()

        return carry

    def grad_copy(m, o):
        return pltpu.make_async_remote_copy(
            src_ref=gsend.at[m],
            dst_ref=grecv.at[m],
            send_sem=gr_send.at[m],
            recv_sem=gr_recv.at[m],
            device_id={"dp": dp_at(o), "tensor": t},
            device_id_type=MESH,
        )

    lax.fori_loop(0, 2 * HEADS, attend, 0)

    def place(b, carry):
        rows = pl.ds(pl.multiple_of(b * 64, 64), 64)
        own, other = res[0, rows, :], res[1, rows, :]
        q_v[0, rows, :] = lax.select(first_own, own, other)
        q_v[1, rows, :] = lax.select(first_own, other, own)
        return carry

    lax.fori_loop(0, ANS // 64, place, 0)
    attn_copy = pltpu.make_async_copy(q_v, attn_hbm, out_sem.at[0])
    attn_copy.start()

    local = (other_index == REACH).astype(f32)
    key_sum = (kg[0, 0] + kg[1, 0] * local) * SCALING
    value_sum = kg[0, 1] + kg[1, 1] * local
    for m, o in enumerate(OFFSETS):
        grad_copy(m, o).wait()
        key_sum = key_sum + grecv[m, :, pl.ds(0, HD)].astype(f32)
        value_sum = value_sum + grecv[m, :, pl.ds(HD, HD)].astype(f32)
    gbuf[0, 0, :, pl.ds(0, HD)] = key_sum.astype(bf16)
    gbuf[0, 0, :, pl.ds(HD, HD)] = value_sum.astype(bf16)

    gather = []
    for n, (cross, by) in enumerate(((1, 2), (0, 2), (1, 1), (0, 1), (1, 3), (0, 3), (1, 0))):
        cp = pltpu.make_async_remote_copy(
            src_ref=gbuf.at[0, 0],
            dst_ref=gbuf.at[cross, (t_count - by) % t_count],
            send_sem=gt_send.at[n],
            recv_sem=gt_recv.at[n],
            device_id={"dp": sib if cross else d, "tensor": t_at(by)},
            device_id_type=MESH,
        )
        cp.start()
        gather.append(cp)

    def widen(by, b, block):
        n = CHUNK
        wk, wv = halves(block, n)
        rows = pl.ds(b * n, n)
        wfull[rows, pl.ds(by * 2 * HD, HD)] = wk
        wfull[rows, pl.ds(by * 2 * HD + HD, HD)] = wv

    for b in range(COLS // CHUNK):
        start = pl.multiple_of(unit * 2 * COLS + b * 2 * CHUNK, 2 * CHUNK)
        widen(0, b, w_v[pl.ds(start, 2 * CHUNK), :])
    for cp in w_copies:
        cp.wait()
    for by in (1, 2, 3):
        for b in range(COLS // CHUNK):
            widen(by, b, wbuf[3 - by, pl.ds(b * 2 * CHUNK, 2 * CHUNK), :])
    for cp in gather:
        cp.wait()

    lhs = jnp.concatenate(
        [jnp.concatenate([gbuf[c, by] for by in range(4)], axis=1) for c in range(2)], axis=0
    )
    otile[...] = dot(lhs, wfull[...], ((1,), (1,))).astype(bf16).reshape(2, PFX, COLS)

    here = pl.ds(pl.multiple_of(unit * COLS, COLS), COLS)
    share = PFX // 4
    outs = []
    for n, (cross, by) in enumerate(((1, 2), (0, 2), (1, 1), (0, 1), (1, 3), (0, 3), (1, 0))):
        to = t_at(by)
        cp = pltpu.make_async_remote_copy(
            src_ref=otile.at[cross, pl.ds(pl.multiple_of(to * share, share), share)],
            dst_ref=pg_hbm.at[:, here],
            send_sem=pg_send.at[n],
            recv_sem=pg_recv.at[n],
            device_id={"dp": sib if cross else d, "tensor": to},
            device_id_type=MESH,
        )
        cp.start()
        outs.append(cp)
    mine = pltpu.make_async_copy(
        otile.at[0, pl.ds(pl.multiple_of(t * share, share), share)], pg_hbm.at[:, here], out_sem.at[1]
    )
    mine.start()
    mine.wait()
    attn_copy.wait()
    for cp in outs:
        cp.wait()


def shards(prefix, kv_weight, ans_query, ans_kv, d_out, branch_prompt):
    t_count, dp_count = lax.axis_size("tensor"), lax.axis_size("dp")
    anyspec = pl.BlockSpec(memory_space=pl.ANY)
    dma = pltpu.SemaphoreType.DMA
    vmem = pltpu.VMEM
    attn, pg = pl.pallas_call(
        functools.partial(kernel, dp_count, t_count),
        out_shape=(
            jax.ShapeDtypeStruct((2, ANS, HEADS * HD), bf16),
            jax.ShapeDtypeStruct((PFX // 4, D), bf16),
        ),
        in_specs=[pl.BlockSpec(memory_space=pltpu.SMEM)] + [anyspec] * 5,
        out_specs=(anyspec, anyspec),
        scratch_shapes=[
            vmem((PFX, D), bf16),
            vmem((2 * D, HD), bf16),
            vmem((2, ANS, HEADS * HD), bf16),
            vmem((2, ANS, HEADS * HD), bf16),
            vmem((2, 2 * ANS, HD), bf16),
            vmem((2 * CHUNK, HD), f32),
            vmem((PFX, 2 * HD), f32),
            vmem((WINDOW, PFX, 2 * HD), bf16),
            vmem((2, PFX + ANS, HD), bf16),
            vmem((2, PFX + ANS, HD), bf16),
            vmem((2, ANS, HEADS * HD), bf16),
            vmem((2, 2, PFX, HD), f32),
            vmem((2 * REACH, PFX, 2 * HD), bf16),
            vmem((2 * REACH, PFX, 2 * HD), bf16),
            vmem((2, 4, PFX, 2 * HD), bf16),
            vmem((3, 2 * COLS, HD), bf16),
            vmem((COLS, 4 * 2 * HD), bf16),
            vmem((2, PFX, COLS), bf16),
            dma((2, CHUNKS)),
            dma((3,)),
            dma((2,)),
            dma((6,)),
            dma((6,)),
            dma((3,)),
            dma((3,)),
            dma((6,)),
            dma((6,)),
            dma((7,)),
            dma((7,)),
            dma((7,)),
            dma((7,)),
        ],
        compiler_params=pltpu.CompilerParams(
            collective_id=0, has_side_effects=True, vmem_limit_bytes=60 * 1024 * 1024
        ),
        name="prefix_step",
    )(
        branch_prompt,
        prefix.reshape(PFX, D),
        kv_weight.reshape(2 * D, HD),
        ans_query.reshape(2, ANS, HEADS * HD),
        ans_kv.reshape(2, 2 * ANS, HD),
        d_out.reshape(2, ANS, HEADS * HD),
    )
    return attn.reshape(2 * ANS, HEADS * HD), pg.reshape(1, PFX // 4, D)


def solution(mesh):
    return jax.shard_map(
        shards,
        mesh=mesh,
        in_specs=(
            P("dp", None, None),
            P(None, None, "tensor"),
            P("dp", "tensor"),
            P("dp", None, "tensor"),
            P("dp", "tensor"),
            P("dp"),
        ),
        out_specs=(P("dp", "tensor"), P("dp", "tensor", None)),
        check_vma=False,
    )
```

time: 141 us -> 62.4 us (0.44)
  the two profiles are of different devices: /device:TPU:102 before, /device:TPU:1 now
where the time goes in v1:
time: 62.4 us; the launch traced here: 62.2 us
  Pallas kernels  57.7 us (92%)
  local copies, waits for them, and re-layouts  3.93 us (6%)
  between operations  0.65 us (1%)
    pallas_call x1, Pallas kernels, shards(): pl.pallas_call(functools.partial(kernel, dp_count, t_count), out_shape=(j...  57.7 us
    unnamed x4, local copies, waits for them, and re-layouts  3.93 us

profile of v1, /device:TPU:1, one launch (start us, length us, event | category | flops | bytes accessed | tf_op | source)
XLA Modules:
  0.0 62.2 jit_solution(15685819884810391346)
XLA Ops:
  0.6 57.7 %prefix_step.1 = (bf16[2,512,1024]{2,1,0:T(8,128)(2,1)}, bf16[32,8192]{1,0:T(8,128)(2,1)}) custom-call(s32[2]{0:T(128)} %bp_ref.1, bf16[128,8192]{1,0:T(8,128)(2,1)} %bitcast.9, bf16[16384,128]{1,0:T(8,128)(2,1)} %bitcast.7, bf16[2,512,1024]{2,1,0:T(8,128)(2,1)} %bitcast.10, bf16[2,1024,128]{2,1,0:T(8,128)(2,1)} %bitcast.12, bf16[2,512,1024]{2,1,0:T(8,128)(2,1)} %bitcast.11), custom_call_target="tpu_custom_call" | custom-call | tf_op jit(solution)/shard_map/prefix_step/pallas_call | solution.py:324
  58.3 0.0 copy-start
  58.3 3.1 %copy.10 = bf16[1024,1024]{1,0:T(8,128)(2,1)} copy(bf16[1024,1024]{1,0:T(8,128)(2,1)} %bitcast.8) | data formatting | bytes 4194304
  61.4 0.0 copy-done
  61.4 0.8 %copy.11 = bf16[1,32,8192]{2,1,0:T(8,128)(2,1)} copy(bf16[1,32,8192]{2,1,0:T(8,128)(2,1)S(1)} %bitcast.13) | data formatting | bytes 1048576
Async XLA Ops:
  58.3 3.1 %copy-start = (bf16[32,8192]{1,0:T(8,128)(2,1)S(1)}, bf16[32,8192]{1,0:T(8,128)(2,1)}, u32[]{:S(2)}) copy-start(bf16[32,8192]{1,0:T(8,128)(2,1)} %get-tuple-element.5) | copy-start | bytes 1572868

commit v2 on v1

v2 whole, which is shorter than its diff:
```python
import functools
import math

import jax
import jax.numpy as jnp
from jax import lax
from jax.experimental import pallas as pl
from jax.experimental.pallas import tpu as pltpu
from jax.sharding import PartitionSpec as P

MESH = pl.DeviceIdType.MESH
HD = 128
PFX = 128
ANS = 512
HEADS = 8
D = 8192
REACH = 3
WINDOW = 2 * REACH + 1
CHUNK = 512
CHUNKS = D // CHUNK
COLS = 1024
ROWS = 256
AT_ONCE = 4
TURNS = 2
FIRST = 2
PASS_AT = 2
AHEAD = 4
X = 4
SCALING = HD ** (-0.5)
LOG2E = math.log2(math.e)
OFFSETS = [o for o in (3, -3, 2, -2, 1, -1)]
f32, bf16 = jnp.float32, jnp.bfloat16


def dot(a, b, dims):
    return lax.dot_general(a, b, (dims, ((), ())), preferred_element_type=f32)


def kernel(
    dp_count,
    t_count,
    bp_ref,
    prefix_hbm,
    w_hbm,
    q_hbm,
    kv_hbm,
    do_hbm,
    res,
    pg,
    prefix_v,
    w_v,
    q_v,
    do_v,
    kv_v,
    wide,
    acc,
    near,
    kfull,
    vt,
    vpre,
    kg,
    gsend,
    grecv,
    gbuf,
    wbuf,
    wfull,
    otile,
    load_sem,
    in_sem,
    kv_send,
    kv_recv,
    w_send,
    w_recv,
    pass_send,
    pass_recv,
    gr_send,
    gr_recv,
    gt_send,
    gt_recv,
    pg_send,
    pg_recv,
):
    d = lax.axis_index("dp")
    t = lax.axis_index("tensor")
    core = lax.rem(d, 2)
    sib = d + 1 - 2 * core
    unit = t * 2 + core

    def dp_at(by):
        return lax.rem(d + by + dp_count, dp_count)

    def t_at(by):
        return lax.rem(t + by, t_count)

    loads = []
    for c in range(CHUNKS):
        cols = pl.ds(c * CHUNK, CHUNK)
        rows = pl.ds(c * 2 * CHUNK, 2 * CHUNK)
        pltpu.make_async_copy(prefix_hbm.at[:, cols], prefix_v.at[:, cols], load_sem.at[0, c]).start()
        pltpu.make_async_copy(w_hbm.at[rows], w_v.at[rows], load_sem.at[1, c]).start()
    for n, (src, dst) in enumerate(((kv_hbm, kv_v), (q_hbm, q_v), (do_hbm, do_v))):
        cp = pltpu.make_async_copy(src, dst, in_sem.at[n])
        cp.start()
        loads.append(cp)

    chip = d // 2
    x, z = lax.rem(chip, X), chip // X
    quarter = lax.rem(z + 2 * x, 4)
    x_next = (z * X + lax.rem(x + 1, X)) * 2 + core
    x_last = (z * X + lax.rem(x + X - 1, X)) * 2 + core
    beside = (dp_at(2 * X), dp_at(-2 * X), x_next, x_last)

    barrier = pltpu.get_barrier_semaphore()
    for o in OFFSETS:
        pl.semaphore_signal(barrier, inc=1, device_id={"dp": dp_at(o), "tensor": t}, device_id_type=MESH)
    for by in range(1, 4):
        pl.semaphore_signal(barrier, inc=1, device_id={"dp": d, "tensor": t_at(by)}, device_id_type=MESH)
        pl.semaphore_signal(barrier, inc=1, device_id={"dp": sib, "tensor": t_at(by)}, device_id_type=MESH)
    for to in beside:
        pl.semaphore_signal(barrier, inc=1, device_id={"dp": to, "tensor": t}, device_id_type=MESH)
    def halves(block, n):
        wide[pl.ds(0, 2 * n), :] = block.astype(f32)
        even = wide[pl.ds(0, n, stride=2), :].astype(bf16)
        odd = wide[pl.ds(1, n, stride=2), :].astype(bf16)
        return even, odd

    acc[...] = jnp.zeros_like(acc)

    def project(c, carry):
        cols = pl.ds(pl.multiple_of(c * CHUNK, CHUNK), CHUNK)
        rows = pl.ds(pl.multiple_of(c * 2 * CHUNK, 2 * CHUNK), 2 * CHUNK)
        pltpu.make_async_copy(prefix_hbm.at[:, cols], prefix_v.at[:, cols], load_sem.at[0, c]).wait()
        pltpu.make_async_copy(w_hbm.at[rows], w_v.at[rows], load_sem.at[1, c]).wait()
        wk, wv = halves(w_v[rows, :], CHUNK)
        acc[...] += dot(prefix_v[:, cols], jnp.concatenate([wk, wv], axis=1), ((1,), (0,)))
        return carry

    lax.fori_loop(0, AHEAD, project, 0)
    pl.semaphore_wait(barrier, 16)
    w_copies = []
    for by in (2, 1, 3):
        to = t_at(by)
        start = (to * 2 + core) * 2 * COLS + quarter * (COLS // 2)
        cp = pltpu.make_async_remote_copy(
            src_ref=w_hbm.at[pl.ds(pl.multiple_of(start, COLS // 2), COLS // 2)],
            dst_ref=wbuf.at[by - 1, quarter],
            send_sem=w_send.at[by - 1],
            recv_sem=w_recv.at[by - 1],
            device_id={"dp": d, "tensor": to},
            device_id_type=MESH,
        )
        cp.start()
        w_copies.append(cp)

    lax.fori_loop(AHEAD, CHUNKS, project, 0)
    near[REACH] = acc[...].astype(bf16)

    kv_copies = []
    for n, o in enumerate(OFFSETS):
        cp = pltpu.make_async_remote_copy(
            src_ref=near.at[REACH],
            dst_ref=near.at[REACH - o],
            send_sem=kv_send.at[n],
            recv_sem=kv_recv.at[n],
            device_id={"dp": dp_at(o), "tensor": t},
            device_id_type=MESH,
        )
        cp.start()
        kv_copies.append(cp)

    def pass_on(by, way):
        half = COLS // 4
        rows = (pl.ds(0, 2 * half), pl.ds(0, 2 * half), pl.ds(0, half), pl.ds(half, half))[way]
        return pltpu.make_async_remote_copy(
            src_ref=wbuf.at[by, quarter, rows],
            dst_ref=wbuf.at[by, quarter, rows],
            send_sem=pass_send.at[by, way],
            recv_sem=pass_recv.at[by, way],
            device_id={"dp": beside[way], "tensor": t},
            device_id_type=MESH,
        )

    first_own = bp_ref[0] == d
    own_slot = jnp.where(first_own, 0, 1)
    other_slot = 1 - own_slot
    other_index = lax.rem(jnp.where(first_own, bp_ref[1], bp_ref[0]) - d + REACH + dp_count, dp_count)

    for cp in loads:
        cp.wait()

    def take_answers(role, slot):
        keys, values = halves(kv_v[slot], ANS)
        kfull[role, pl.ds(PFX, ANS), :] = keys
        vt[role, :, pl.ds(PFX, ANS)] = values.T

    def take_prefix(role, block):
        kfull[role, pl.ds(0, PFX), :] = block[:, :HD]
        vpre[role] = block[:, HD:]
        vt[role, :, pl.ds(0, PFX)] = block[:, HD:].T

    take_answers(0, own_slot)
    take_answers(1, other_slot)
    take_prefix(0, near[REACH])
    kg[...] = jnp.zeros_like(kg)

    def attend(n, carry):
        @pl.when(n == FIRST)
        def _():
            for cp in kv_copies:
                cp.wait()
            take_prefix(1, near[jnp.minimum(other_index, WINDOW - 1)])

        @pl.when(n == PASS_AT)
        def _():
            for cp in w_copies:
                cp.wait()
            for by in range(3):
                for way in range(4):
                    pass_on(by, way).start()

        is_other = (n >= FIRST) & (n < FIRST + TURNS)
        role = jnp.where(is_other, 1, 0)
        turn = jnp.where(n < FIRST, n, jnp.where(is_other, n - FIRST, n - TURNS))
        slot = jnp.where(is_other, other_slot, own_slot)
        causal = lax.broadcasted_iota(jnp.int32, (HD, HD), 0) <= lax.broadcasted_iota(jnp.int32, (HD, HD), 1)

        def place_of(b):
            lanes = pl.ds(pl.multiple_of((turn * AT_ONCE + b // 2) * HD, HD), HD)
            return pl.ds((b % 2) * ROWS, ROWS), lanes, PFX + (b % 2 + 1) * ROWS

        def scores(b):
            rows, lanes, end = place_of(b)
            return dot(kfull[role, pl.ds(0, end), :], q_v[slot, rows, lanes], ((1,), (1,)))

        def softmax(s):
            fulls, halfs = [], []
            for part in range(ROWS // HD):
                end = s.shape[0] - ROWS + (part + 1) * HD
                own = s[:end, part * HD : (part + 1) * HD]
                tail = jnp.where(causal, own[end - HD :], -jnp.inf)
                own = jnp.concatenate([own[: end - HD], tail], axis=0)
                top = jnp.max(own, axis=0, keepdims=True)
                e = jnp.exp2((own - top) * (SCALING * LOG2E))
                full = e * (1.0 / jnp.sum(e, axis=0, keepdims=True))
                fulls.append(full[:PFX])
                half = full.astype(bf16)
                if end < s.shape[0]:
                    half = jnp.concatenate([half, jnp.zeros((s.shape[0] - end, HD), bf16)], axis=0)
                halfs.append(half)
            return jnp.concatenate(fulls, axis=1), jnp.concatenate(halfs, axis=1)

        def rest(b, full, half):
            rows, lanes, end = place_of(b)
            q, do = q_v[slot, rows, lanes], do_v[slot, rows, lanes]
            ctx = dot(vt[role, :, pl.ds(0, end)], half, ((1,), (0,)))
            res[role, rows, lanes] = ctx.astype(bf16).T
            grad = dot(vpre[role], do, ((1,), (1,)))
            delta = jnp.sum(do.T.astype(f32) * ctx, axis=0, keepdims=True)
            sg = (full * (grad - delta)).astype(bf16)
            kg[role, 0] += dot(sg, q, ((1,), (0,)))
            kg[role, 1] += dot(half[:PFX], do, ((1,), (0,)))

        count = 2 * AT_ONCE
        waiting = scores(0)
        done = None
        for b in range(count):
            now = waiting
            if b + 1 < count:
                waiting = scores(b + 1)
            probs = softmax(now)
            if done is not None:
                rest(b - 1, *done)
            done = probs
        rest(count - 1, *done)

        @pl.when(n == FIRST + TURNS - 1)
        def _():
            key_grad = (kg[1, 0] * SCALING).astype(bf16)
            value_grad = kg[1, 1].astype(bf16)
            zero = jnp.zeros((PFX, HD), bf16)
            for m, o in enumerate(OFFSETS):
                keep = other_index == o + REACH
                gsend[m, :, pl.ds(0, HD)] = lax.select(keep, key_grad, zero)
                gsend[m, :, pl.ds(HD, HD)] = lax.select(keep, value_grad, zero)
                grad_copy(m, o).start()

        return carry

    def grad_copy(m, o):
        return pltpu.make_async_remote_copy(
            src_ref=gsend.at[m],
            dst_ref=grecv.at[m],
            send_sem=gr_send.at[m],
            recv_sem=gr_recv.at[m],
            device_id={"dp": dp_at(o), "tensor": t},
            device_id_type=MESH,
        )

    lax.fori_loop(0, 2 * TURNS, attend, 0)

    def widen(by, b, block, part=None):
        n = CHUNK if part is None else CHUNK // 2
        wk, wv = halves(block, n)
        rows = pl.ds(b * CHUNK + (part or 0) * n, n)
        wfull[rows, pl.ds(by * 2 * HD, HD)] = wk
        wfull[rows, pl.ds(by * 2 * HD + HD, HD)] = wv

    for b in range(COLS // CHUNK):
        start = pl.multiple_of(unit * 2 * COLS + b * 2 * CHUNK, 2 * CHUNK)
        widen(0, b, w_v[pl.ds(start, 2 * CHUNK), :])
    local = (other_index == REACH).astype(f32)
    key_sum = (kg[0, 0] + kg[1, 0] * local) * SCALING
    value_sum = kg[0, 1] + kg[1, 1] * local
    for m, o in enumerate(OFFSETS):
        grad_copy(m, o).wait()
        key_sum = key_sum + grecv[m, :, pl.ds(0, HD)].astype(f32)
        value_sum = value_sum + grecv[m, :, pl.ds(HD, HD)].astype(f32)
    gbuf[0, 0, :, pl.ds(0, HD)] = key_sum.astype(bf16)
    gbuf[0, 0, :, pl.ds(HD, HD)] = value_sum.astype(bf16)

    def gather(cross, by):
        n = cross * 4 + by
        here_at = (t_count - by) % t_count
        return pltpu.make_async_remote_copy(
            src_ref=gbuf.at[0, by] if cross else gbuf.at[0, 0],
            dst_ref=gbuf.at[1, by] if cross else gbuf.at[0, here_at],
            send_sem=gt_send.at[n],
            recv_sem=gt_recv.at[n],
            device_id={"dp": sib, "tensor": t} if cross else {"dp": d, "tensor": t_at(by)},
            device_id_type=MESH,
        )

    for by in (2, 1, 3):
        gather(0, by).start()
    gather(1, 0).start()
    for by in (1, 3, 2):
        gather(0, (t_count - by) % t_count).wait_recv()
        gather(1, by).start()
    for by in range(3):
        for way in range(4):
            pass_on(by, way).wait()
    for by in (1, 2, 3):
        for b in range(COLS // CHUNK):
            for part in range(2):
                widen(by, b, wbuf[3 - by, 2 * b + part], part)
    for by in (1, 2, 3):
        gather(0, by).wait_send()
    for by in range(4):
        gather(1, by).wait()

    lhs = jnp.concatenate(
        [jnp.concatenate([gbuf[c, by] for by in range(4)], axis=1) for c in range(2)], axis=0
    )
    otile[...] = dot(lhs, wfull[...], ((1,), (1,))).astype(bf16).reshape(2, PFX, COLS)

    here = pl.ds(pl.multiple_of(unit * COLS, COLS), COLS)
    share = PFX // 4
    outs = []
    for n, (cross, by) in enumerate(((1, 2), (0, 2), (1, 1), (0, 1), (1, 3), (0, 3), (1, 0))):
        to = t_at(by)
        cp = pltpu.make_async_remote_copy(
            src_ref=otile.at[cross, pl.ds(pl.multiple_of(to * share, share), share)],
            dst_ref=pg.at[:, here],
            send_sem=pg_send.at[n],
            recv_sem=pg_recv.at[n],
            device_id={"dp": sib if cross else d, "tensor": to},
            device_id_type=MESH,
        )
        cp.start()
        outs.append(cp)
    pg[:, here] = otile[0, pl.ds(pl.multiple_of(t * share, share), share), :]
    for cp in outs:
        cp.wait()


def put_out(bp_ref, res, pg, attn_hbm, pg_hbm, sem):
    own_slot = jnp.where(bp_ref[0] == lax.axis_index("dp"), 0, 1)
    copies = [
        pltpu.make_async_copy(res.at[0], attn_hbm.at[own_slot], sem.at[0]),
        pltpu.make_async_copy(res.at[1], attn_hbm.at[1 - own_slot], sem.at[1]),
        pltpu.make_async_copy(pg, pg_hbm, sem.at[2]),
    ]
    for cp in copies:
        cp.start()
    for cp in copies:
        cp.wait()


def shards(prefix, kv_weight, ans_query, ans_kv, d_out, branch_prompt):
    t_count, dp_count = lax.axis_size("tensor"), lax.axis_size("dp")
    hbm = pl.BlockSpec(memory_space=pltpu.HBM)
    whole = pl.BlockSpec(memory_space=pltpu.VMEM)
    dma = pltpu.SemaphoreType.DMA
    vmem = pltpu.VMEM
    attn, pg = pl.pallas_call(
        functools.partial(kernel, dp_count, t_count),
        out_shape=(
            pltpu.VMEM((2, ANS, HEADS * HD), bf16),
            pltpu.VMEM((PFX // 4, D), bf16),
        ),
        in_specs=[pl.BlockSpec(memory_space=pltpu.SMEM)] + [hbm] * 5,
        out_specs=(whole, whole),
        scratch_shapes=[
            vmem((PFX, D), bf16),
            vmem((2 * D, HD), bf16),
            vmem((2, ANS, HEADS * HD), bf16),
            vmem((2, ANS, HEADS * HD), bf16),
            vmem((2, 2 * ANS, HD), bf16),
            vmem((2 * CHUNK, HD), f32),
            vmem((PFX, 2 * HD), f32),
            vmem((WINDOW, PFX, 2 * HD), bf16),
            vmem((2, PFX + ANS, HD), bf16),
            vmem((2, HD, PFX + ANS), bf16),
            vmem((2, PFX, HD), bf16),
            vmem((2, 2, PFX, HD), f32),
            vmem((2 * REACH, PFX, 2 * HD), bf16),
            vmem((2 * REACH, PFX, 2 * HD), bf16),
            vmem((2, 4, PFX, 2 * HD), bf16),
            vmem((3, 4, COLS // 2, HD), bf16),
            vmem((COLS, 4 * 2 * HD), bf16),
            vmem((2, PFX, COLS), bf16),
            dma((2, CHUNKS)),
            dma((3,)),
            dma((6,)),
            dma((6,)),
            dma((3,)),
            dma((3,)),
            dma((3, 4)),
            dma((3, 4)),
            dma((6,)),
            dma((6,)),
            dma((8,)),
            dma((8,)),
            dma((7,)),
            dma((7,)),
        ],
        compiler_params=pltpu.CompilerParams(
            collective_id=0, has_side_effects=True, vmem_limit_bytes=58 * 1024 * 1024
        ),
        name="prefix_step",
    )(
        branch_prompt,
        prefix.reshape(PFX, D),
        kv_weight.reshape(2 * D, HD),
        ans_query.reshape(2, ANS, HEADS * HD),
        ans_kv.reshape(2, 2 * ANS, HD),
        d_out.reshape(2, ANS, HEADS * HD),
    )
    attn, pg = pl.pallas_call(
        put_out,
        out_shape=(
            jax.ShapeDtypeStruct((2, ANS, HEADS * HD), bf16),
            jax.ShapeDtypeStruct((PFX // 4, D), bf16),
        ),
        in_specs=[pl.BlockSpec(memory_space=pltpu.SMEM), whole, whole],
        out_specs=(hbm, hbm),
        scratch_shapes=[dma((3,))],
        name="put_out",
    )(branch_prompt, pltpu.with_memory_space_constraint(attn, pltpu.VMEM), pltpu.with_memory_space_constraint(pg, pltpu.VMEM))
    return attn.reshape(2 * ANS, HEADS * HD), pg.reshape(1, PFX // 4, D)


def solution(mesh):
    return jax.shard_map(
        shards,
        mesh=mesh,
        in_specs=(
            P("dp", None, None),
            P(None, None, "tensor"),
            P("dp", "tensor"),
            P("dp", None, "tensor"),
            P("dp", "tensor"),
            P("dp"),
        ),
        out_specs=(P("dp", "tensor"), P("dp", "tensor", None)),
        check_vma=False,
    )
```

time: 62.4 us -> 54.2 us (0.87)
  Pallas kernels: 57.7 us -> 53.5 us
  local copies, waits for them, and re-layouts: 3.93 us -> 0 us
    pallas_call x1 -> x2, Pallas kernels: 57.7 us -> 53.5 us  [the longest x1 51.3 us: shards(): pl.pallas_call(functools.partial(kernel, dp_count, t_count), out_shape=(p...]
    unnamed x4 -> x0, local copies, waits for them, and re-layouts: 3.93 us -> none
where the time goes in v2:
time: 54.2 us; the launch traced here: 54.1 us
  Pallas kernels  53.5 us (99%)
  between operations  0.64 us (1%)
    pallas_call x1, Pallas kernels, shards(): pl.pallas_call(functools.partial(kernel, dp_count, t_count), out_shape=(p...  51.3 us
    pallas_call x1, Pallas kernels, shards(): pl.pallas_call(put_out, out_shape=(jax.ShapeDtypeStruct((2, ANS, HEADS *...  2.19 us

profile of v2, /device:TPU:1, one launch (start us, length us, event | category | flops | bytes accessed | tf_op | source)
XLA Modules:
  0.0 54.1 jit_solution(6283784754946037963)
XLA Ops:
  0.6 51.3 %prefix_step.1 = (bf16[2,512,1024]{2,1,0:T(8,128)(2,1)S(1)}, bf16[32,8192]{1,0:T(8,128)(2,1)S(1)}) custom-call(s32[2]{0:T(128)} %bp_ref.3, bf16[128,8192]{1,0:T(8,128)(2,1)} %bitcast.8, bf16[16384,128]{1,0:T(8,128)(2,1)} %bitcast.7, bf16[2,512,1024]{2,1,0:T(8,128)(2,1)} %bitcast.9, bf16[2,1024,128]{2,1,0:T(8,128)(2,1)} %bitcast.11, ...), custom_call_target="tpu_custom_call" | custom-call | tf_op jit(solution)/shard_map/prefix_step/pallas_call | solution.py:395
  51.9 2.2 %put_out.1 = (bf16[2,512,1024]{2,1,0:T(8,128)(2,1)}, bf16[32,8192]{1,0:T(8,128)(2,1)}) custom-call(s32[2]{0:T(128)} %bp_ref.3, bf16[2,512,1024]{2,1,0:T(8,128)(2,1)S(1)} %get-tuple-element.6.res, bf16[32,8192]{1,0:T(8,128)(2,1)S(1)} %get-tuple-element.7.pg), custom_call_target="tpu_custom_call" | custom-call | tf_op jit(solution)/shard_map/put_out/pallas_call | solution.py:449

commit v3 on v2

--- a/solution.py
+++ b/solution.py
@@ -25,6 +25,8 @@
 FIRST = 2
 PASS_AT = 2
 AHEAD = 4
+LOAD_AT = 9
+PIECES = 2
 X = 4
 SCALING = HD ** (-0.5)
 LOG2E = math.log2(math.e)
@@ -99,9 +101,7 @@
         pltpu.make_async_copy(prefix_hbm.at[:, cols], prefix_v.at[:, cols], load_sem.at[0, c]).start()
         pltpu.make_async_copy(w_hbm.at[rows], w_v.at[rows], load_sem.at[1, c]).start()
     for n, (src, dst) in enumerate(((kv_hbm, kv_v), (q_hbm, q_v), (do_hbm, do_v))):
-        cp = pltpu.make_async_copy(src, dst, in_sem.at[n])
-        cp.start()
-        loads.append(cp)
+        loads.append(pltpu.make_async_copy(src, dst, in_sem.at[n]))
 
     chip = d // 2
     x, z = lax.rem(chip, X), chip // X
@@ -152,7 +152,10 @@
         cp.start()
         w_copies.append(cp)
 
-    lax.fori_loop(AHEAD, CHUNKS, project, 0)
+    lax.fori_loop(AHEAD, LOAD_AT, project, 0)
+    for cp in loads:
+        cp.start()
+    lax.fori_loop(LOAD_AT, CHUNKS, project, 0)
     near[REACH] = acc[...].astype(bf16)
 
     kv_copies = []
@@ -210,13 +213,19 @@
                 cp.wait()
             take_prefix(1, near[jnp.minimum(other_index, WINDOW - 1)])
 
-        @pl.when(n == PASS_AT)
+        @pl.when(n == PASS_AT - 1)
         def _():
-            for cp in w_copies:
+            for cp in w_copies[1:]:
                 cp.wait()
-            for by in range(3):
+            for by in (0, 2):
                 for way in range(4):
                     pass_on(by, way).start()
+
+        @pl.when(n == PASS_AT + 1)
+        def _():
+            w_copies[0].wait()
+            for way in range(4):
+                pass_on(1, way).start()
 
         is_other = (n >= FIRST) & (n < FIRST + TURNS)
         role = jnp.where(is_other, 1, 0)
@@ -351,24 +360,28 @@
     lhs = jnp.concatenate(
         [jnp.concatenate([gbuf[c, by] for by in range(4)], axis=1) for c in range(2)], axis=0
     )
-    otile[...] = dot(lhs, wfull[...], ((1,), (1,))).astype(bf16).reshape(2, PFX, COLS)
-
-    here = pl.ds(pl.multiple_of(unit * COLS, COLS), COLS)
     share = PFX // 4
+    mine = pl.ds(pl.multiple_of(t * share, share), share)
     outs = []
-    for n, (cross, by) in enumerate(((1, 2), (0, 2), (1, 1), (0, 1), (1, 3), (0, 3), (1, 0))):
-        to = t_at(by)
-        cp = pltpu.make_async_remote_copy(
-            src_ref=otile.at[cross, pl.ds(pl.multiple_of(to * share, share), share)],
-            dst_ref=pg.at[:, here],
-            send_sem=pg_send.at[n],
-            recv_sem=pg_recv.at[n],
-            device_id={"dp": sib if cross else d, "tensor": to},
-            device_id_type=MESH,
-        )
-        cp.start()
-        outs.append(cp)
-    pg[:, here] = otile[0, pl.ds(pl.multiple_of(t * share, share), share), :]
+    for piece in range(PIECES):
+        width = COLS // PIECES
+        part = pl.ds(piece * width, width)
+        here = pl.ds(pl.multiple_of(unit * COLS + piece * width, width), width)
+        rows = dot(lhs, wfull[part, :], ((1,), (1,))).astype(bf16)
+        otile[:, :, part] = rows.reshape(2, PFX, width)
+        for n, (cross, by) in enumerate(((1, 2), (0, 2), (1, 1), (0, 1), (1, 3), (0, 3), (1, 0))):
+            to = t_at(by)
+            cp = pltpu.make_async_remote_copy(
+                src_ref=otile.at[cross, pl.ds(pl.multiple_of(to * share, share), share), part],
+                dst_ref=pg.at[:, here],
+                send_sem=pg_send.at[piece, n],
+                recv_sem=pg_recv.at[piece, n],
+                device_id={"dp": sib if cross else d, "tensor": to},
+                device_id_type=MESH,
+            )
+            cp.start()
+            outs.append(cp)
+        pg[:, here] = otile[0, mine, part]
     for cp in outs:
         cp.wait()
 
@@ -431,8 +444,8 @@
             dma((6,)),
             dma((8,)),
             dma((8,)),
-            dma((7,)),
-            dma((7,)),
+            dma((PIECES, 7)),
+            dma((PIECES, 7)),
         ],
         compiler_params=pltpu.CompilerParams(
             collective_id=0, has_side_effects=True, vmem_limit_bytes=58 * 1024 * 1024

time: 54.2 us -> 53.1 us (0.980)
  Pallas kernels: 53.5 us -> 52.3 us
    pallas_call x1, Pallas kernels: 51.3 us -> 50.2 us  [shards(): pl.pallas_call(functools.partial(kernel, dp_count, t_count), out_shape=(p...]
where the time goes in v3:
time: 53.1 us; the launch traced here: 53 us
  Pallas kernels  52.3 us (98%)
  between operations  0.64 us (1%)
    pallas_call x1, Pallas kernels, shards(): pl.pallas_call(functools.partial(kernel, dp_count, t_count), out_shape=(p...  50.2 us
    pallas_call x1, Pallas kernels, shards(): pl.pallas_call(put_out, out_shape=(jax.ShapeDtypeStruct((2, ANS, HEADS *...  2.19 us

profile of v3, /device:TPU:1, one launch (start us, length us, event | category | flops | bytes accessed | tf_op | source)
XLA Modules:
  0.0 53.0 jit_solution(15945422387977478660)
XLA Ops:
  0.6 50.2 %prefix_step.1 = (bf16[2,512,1024]{2,1,0:T(8,128)(2,1)S(1)}, bf16[32,8192]{1,0:T(8,128)(2,1)S(1)}) custom-call(s32[2]{0:T(128)} %bp_ref.3, bf16[128,8192]{1,0:T(8,128)(2,1)} %bitcast.8, bf16[16384,128]{1,0:T(8,128)(2,1)} %bitcast.7, bf16[2,512,1024]{2,1,0:T(8,128)(2,1)} %bitcast.9, bf16[2,1024,128]{2,1,0:T(8,128)(2,1)} %bitcast.11, ...), custom_call_target="tpu_custom_call" | custom-call | tf_op jit(solution)/shard_map/prefix_step/pallas_call | solution.py:408
  50.8 2.2 %put_out.1 = (bf16[2,512,1024]{2,1,0:T(8,128)(2,1)}, bf16[32,8192]{1,0:T(8,128)(2,1)}) custom-call(s32[2]{0:T(128)} %bp_ref.3, bf16[2,512,1024]{2,1,0:T(8,128)(2,1)S(1)} %get-tuple-element.6.res, bf16[32,8192]{1,0:T(8,128)(2,1)S(1)} %get-tuple-element.7.pg), custom_call_target="tpu_custom_call" | custom-call | tf_op jit(solution)/shard_map/put_out/pallas_call | solution.py:462
